TPU v7x, 256 devices: a whole 4x4x8 slice. The times are simulated.
256 devices in a mesh: rep: 8 (over x, core), shard: 32 (over y, z).
Axes of the slice: x: 4, y: 4, z: 8, core: 2. Of those that a mesh axis runs over, the one named last changes fastest.
Arguments:
- grads: float32 [8, 32, 64, 128, 128], P('rep', 'shard'), may hold values from -24 to 24
- counts: int32 [8, 32, 64, 128], P('rep', 'shard'), may hold values from 0 to 5
- block_owner: int32 [8, 32, 64, 1], P('rep', 'shard'), may hold values from 0 to 31; in each aligned block of 64 rows (0 to 63, 64 to 127, ..., all dimensions but the last counted through in order) at most 4 rows name the same one
- block_local: int32 [8, 32, 64], P('rep', 'shard'), may hold values from 0 to 63
Outputs:
- clipped: float32 [2048, 128, 128], P('shard', 'rep')
Inputs may be any that keep to these rules, and one draw needn't show every extreme that they name: `block_owner`: among the 64 blocks of one device no owner is named more than 4 times, a bound that some block reaches.
All inputs are finite; a program needn't handle non-finite values.
Results may differ from a plain program's by a relative error of at most 0.0003.
Values sent between devices are 32-bit elements; how exact they have to be, the bound alone decides.
A program may use at most 128 MiB of HBM per device.

v0:
```python
import math

import jax
import jax.numpy as jnp
from jax import lax
from jax.sharding import Mesh
from jax.sharding import PartitionSpec as P

BLK_SHARD = 64
CAP = 4
SHARD = ("shard_0", "shard_1")
REP = ("rep_0", "rep_1")
REP_SHARD = ("rep_0", "rep_1", "shard_0", "shard_1")


def sent_together(arrays, axis, dim, along):
    columns = [a.reshape(*a.shape[:along], -1) for a in arrays]
    both = jnp.concatenate(columns, axis=along)
    whole, at, gathered = (lax.psum_scatter(both, axis, scatter_dimension=dim, tiled=True), 0, [])
    for a, column in zip(arrays, columns):
        piece = whole[..., at : at + column.shape[along]]
        gathered.append(piece.reshape(*piece.shape[:along], *a.shape[along:]))
        at += column.shape[along]
    return tuple(gathered)


def one_axis_at_a_time(value, axes):
    for axis in axes:
        value = lax.psum(value, axis)
    return value


def accumulate(values, tallies, indices, owned):
    slots = indices.shape[0]
    onehot = (jnp.arange(owned, dtype=jnp.int32)[:, None] == indices[None, :]).astype(jnp.float32)
    sums = jnp.dot(
        onehot,
        values.reshape(slots, -1),
        precision=lax.Precision.HIGHEST,
        preferred_element_type=jnp.float32,
    )
    totals = jnp.dot(
        onehot, tallies, precision=lax.Precision.HIGHEST, preferred_element_type=jnp.float32
    )
    return (sums.reshape(owned, values.shape[1], values.shape[2]), totals)


def local(grads, counts, block_owner, block_local):
    nshard = lax.axis_size(SHARD)
    nblocks = grads.shape[2]
    rows = grads.shape[3]
    width = grads.shape[4]
    owners = block_owner.reshape(nblocks)
    local_ids = block_local.reshape(nblocks)
    blocks = grads.reshape(nblocks, rows, width)
    tallies = counts.reshape(nblocks, rows)
    masked = jnp.where(tallies[..., None] > 0, blocks, jnp.float32(0.0))
    owner_hot = (owners[:, None] == jnp.arange(nshard, dtype=jnp.int32)[None, :]).astype(jnp.int32)
    ranking = jnp.sum(jnp.cumsum(owner_hot, axis=0) * owner_hot, axis=1) - 1
    slot_of = owners * CAP + ranking
    send_vals = jnp.zeros((nshard * CAP, rows, width), jnp.float32).at[slot_of].set(masked)
    send_vals = send_vals.reshape(nshard, CAP, rows, width)
    send_cnts = (
        jnp.zeros((nshard * CAP, rows), jnp.float32).at[slot_of].set(tallies.astype(jnp.float32))
    )
    send_cnts = send_cnts.reshape(nshard, CAP, rows)
    send_ids = (
        jnp.full((nshard * CAP,), -1, jnp.int32).at[slot_of].set(local_ids).reshape(nshard, CAP)
    )
    got_vals, got_cnts, got_ids = (
        lax.all_to_all(send_vals, SHARD, split_axis=0, concat_axis=0, tiled=True),
        lax.all_to_all(send_cnts, SHARD, split_axis=0, concat_axis=0, tiled=True),
        lax.all_to_all(send_ids, SHARD, split_axis=0, concat_axis=0, tiled=True),
    )
    sums, totals = accumulate(
        got_vals.reshape(-1, rows, width),
        got_cnts.reshape(-1, rows),
        got_ids.reshape(-1),
        BLK_SHARD,
    )
    sums, totals = sent_together((sums, totals), REP, 1, 2)
    mean = sums / jnp.maximum(totals, jnp.float32(1.0))[..., None]
    norm2 = one_axis_at_a_time(jnp.sum(mean * mean), REP_SHARD)
    limit = jnp.float32(0.2 * math.sqrt(BLK_SHARD * nshard * rows * width))
    scale = jnp.minimum(jnp.float32(1.0), limit / jnp.sqrt(norm2 + jnp.float32(1e-06)))
    return mean * scale


def solution(mesh):
    finer = Mesh(mesh.devices.reshape(4, 2, 4, 8), ("rep_0", "rep_1", "shard_0", "shard_1"))
    return jax.shard_map(
        local,
        mesh=finer,
        in_specs=(
            P(REP, SHARD, None, None, None),
            P(REP, SHARD, None, None),
            P(REP, SHARD, None, None),
            P(REP, SHARD, None),
        ),
        out_specs=P(SHARD, REP, None),
        check_vma=False,
    )
```

profile of v0, /device:TPU:1, one launch (start us, length us, event | category | flops | bytes accessed | tf_op | source)
XLA Modules:
  0.0 390.6 jit_solution(1118153710356190807)
XLA Ops:
  6.5 0.7 fusion.5
  7.3 0.1 reduce_window_sum.11
  7.4 0.8 select_reduce_fusion
  8.2 0.7 fusion.11
  8.9 0.9 scatter_custom_fusion
  9.8 0.7 all_to_all.12
  10.5 12.0 %all-to-all-start = ((s32[32,1,4]{2,1,0:T(1,128)}), s32[32,1,4]{2,1,0:T(1,128)S(1)}, u32[]{:S(2)}, u32[]{:S(2)}) async-start(s32[32,1,4]{2,1,0:T(1,128)} %bitcast.5), calls=%async_computation | async-start | bytes 32768 | tf_op jit(solution)/shard_map/all_to_all | solution.py:73
  22.5 0.8 compare_bitcast_fusion
  23.3 1.5 scatter_custom_fusion.2
  24.8 6.3 %all-to-all-done = s32[32,1,4]{2,1,0:T(1,128)S(1)} async-done(((s32[32,1,4]{2,1,0:T(1,128)}), s32[32,1,4]{2,1,0:T(1,128)S(1)}, u32[]{:S(2)}, u32[]{:S(2)}) %all-to-all-start) | async-done | bytes 544 | tf_op jit(solution)/shard_map/all_to_all | solution.py:73
  31.2 3.9 all-to-all-start.2
  35.0 5.3 %bitcast_select_fusion = f32[64,128,128]{2,1,0:T(8,128)} fusion(f32[1,1,64,128,128]{4,3,2,1,0:T(8,128)} %param.4, pred[64,128]{1,0:T(8,128)(4,1)S(1)} %compare_bitcast_fusion), kind=kLoop, calls=%fused_computation.5 | loop fusion | flops 1048576 | bytes 8396800 | tf_op jit(solution)/shard_map/jit(_where)/select_n | solution.py:57
  40.3 4.3 %broadcast_in_dim.28 = f32[128,128,128]{2,1,0:T(8,128)} broadcast(f32[]{:T(128)} %constant.12.clone.1), dimensions={} | broadcast | bytes 8388612 | tf_op jit(solution)/shard_map/broadcast_in_dim | solution.py:61
  44.5 12.0 %scatter_fusion = f32[128,128,128]{2,1,0:T(8,128)} fusion(f32[128,128,128]{2,1,0:T(8,128)} %broadcast_in_dim.28, s32[64]{0:T(128)S(1)} %fusion.11, f32[64,128,128]{2,1,0:T(8,128)} %bitcast_select_fusion), kind=kCustom, calls=%fused_computation.1 | custom fusion | bytes 12583168 | tf_op jit(solution)/shard_map/scatter | solution.py:61
  56.5 0.0 all-to-all-done.2
  56.5 9.4 %all-to-all-start.1 = ((f32[32,4,128,128]{3,2,1,0:T(8,128)}), f32[32,4,128,128]{3,2,1,0:T(8,128)}, u32[]{:S(2)}, u32[]{:S(2)}) async-start(f32[32,4,128,128]{3,2,1,0:T(8,128)} %bitcast.37), calls=%async_computation.1 | async-start | bytes 16777216 | tf_op jit(solution)/shard_map/all_to_all | solution.py:71
  65.9 0.2 reduce-scatter.2.cloned.1.call-start
  66.1 0.5 broadcast.64
  66.6 0.7 reduce.5
  67.3 0.1 eq.35
  67.4 0.2 convolution_bitcast_fusion
  67.6 4.4 %copy.12 = f32[64,128,1]{2,0,1:T(8,128)} copy(f32[64,128,1]{1,0,2:T(8,128)S(1)} %convolution_bitcast_fusion) | data formatting | bytes 65536 | tf_op jit(solution)/shard_map/reshape | solution.py:17
  72.0 176.9 %all-to-all-done.1 = f32[32,4,128,128]{3,2,1,0:T(8,128)} async-done(((f32[32,4,128,128]{3,2,1,0:T(8,128)}), f32[32,4,128,128]{3,2,1,0:T(8,128)}, u32[]{:S(2)}, u32[]{:S(2)}) %all-to-all-start.1) | async-done | bytes 8388640 | tf_op jit(solution)/shard_map/all_to_all | solution.py:71
  248.9 13.1 %copy.16 = f32[16,8,128,128]{3,1,2,0:T(8,128)} copy(f32[16,8,128,128]{3,2,1,0:T(8,128)} %bitcast.17) | data formatting | bytes 16777216
  262.0 9.0 %copy.11 = f32[16384,128]{1,0:T(8,128)} copy(f32[16384,128]{0,1:T(8,128)} %bitcast.39) | data formatting | bytes 16777216 | tf_op jit(solution)/shard_map/dot_general | solution.py:36
  271.0 0.0 copy-start
  271.0 7.5 %fusion.7 = f32[64,128,128]{2,0,1:T(8,128)S(1)} fusion(f32[128,128,128]{2,1,0:T(8,128)} %bitcast.38, s32[128]{0:T(128)S(1)} %eq.35), kind=kOutput, calls=%fused_computation.21 | convolution fusion | flops 1610620928 | bytes 12583424 | tf_op jit(solution)/shard_map/dot_general | solution.py:36
  278.5 0.0 copy-done
  278.5 4.2 %pad_maximum_fusion = f32[64,128,129]{2,0,1:T(8,128)} fusion(f32[64,128,1]{2,0,1:T(8,128)S(1)} %copy-done, f32[64,128,128]{2,0,1:T(8,128)S(1)} %fusion.7), kind=kLoop, calls=%fused_computation.4 | loop fusion | flops 1056768 | bytes 8454144 | tf_op jit(solution)/shard_map/concatenate | solution.py:18
  282.7 0.0 reduce-scatter.2.cloned.1.call-update
  282.7 58.4 %reduce-scatter.2.cloned.1.call-done = f32[64,16,129]{2,0,1:T(8,128)} async-done(((f32[64,128,129]{2,0,1:T(8,128)}), f32[64,16,129]{2,0,1:T(8,128)}) %reduce-scatter.2.cloned.1.call-update) | async-done | bytes 528400 | tf_op jit(solution)/shard_map/reduce_scatter | solution.py:19
  341.1 1.2 fusion
  342.3 1.9 multiply_reduce_fusion
  344.2 8.1 %psum.28 = f32[]{:T(128)} all-reduce(f32[]{:T(128)} %multiply_reduce_fusion), channel_id=1, replica_groups=mesh['rep_0'=4,'rep_1'=2,'shard_0'=4,'shard_1'=8] {'rep_0'}, use_global_device_ids=true, to_apply=%region_7.8 | all-reduce | flops 1 | bytes 8 | tf_op jit(solution)/shard_map/psum | solution.py:29
  352.3 5.0 %psum.29 = f32[]{:T(128)} all-reduce(f32[]{:T(128)} %psum.28), channel_id=1, replica_groups=mesh['rep_0'=4,'rep_1'=2,'shard_0'=4,'shard_1'=8] {'rep_1'}, use_global_device_ids=true, to_apply=%region_8.9 | all-reduce | flops 1 | bytes 8 | tf_op jit(solution)/shard_map/psum | solution.py:29
  357.3 9.1 %psum.30 = f32[]{:T(128)} all-reduce(f32[]{:T(128)} %psum.29), channel_id=1, replica_groups=mesh['rep_0'=4,'rep_1'=2,'shard_0'=4,'shard_1'=8] {'shard_0'}, use_global_device_ids=true, to_apply=%region_9.10 | all-reduce | flops 1 | bytes 8 | tf_op jit(solution)/shard_map/psum | solution.py:29
  366.4 14.3 %psum.31 = f32[]{:T(128)} all-reduce(f32[]{:T(128)} %psum.30), channel_id=1, replica_groups=mesh['rep_0'=4,'rep_1'=2,'shard_0'=4,'shard_1'=8] {'shard_1'}, use_global_device_ids=true, to_apply=%region_10.11 | all-reduce | flops 1 | bytes 8 | tf_op jit(solution)/shard_map/psum | solution.py:29
  381.4 1.2 broadcast_multiply_fusion
  382.7 1.1 copy.13
Async XLA Ops:
  10.5 20.7 %all-to-all-start = ((s32[32,1,4]{2,1,0:T(1,128)}), s32[32,1,4]{2,1,0:T(1,128)S(1)}, u32[]{:S(2)}, u32[]{:S(2)}) async-start(s32[32,1,4]{2,1,0:T(1,128)} %bitcast.5), calls=%async_computation | async-start | bytes 32768 | tf_op jit(solution)/shard_map/all_to_all | solution.py:73
  31.2 25.3 %all-to-all-start.2 = ((f32[32,4,128]{2,1,0:T(4,128)}), f32[32,4,128]{2,1,0:T(4,128)S(1)}, u32[]{:S(2)}, u32[]{:S(2)}) async-start(f32[32,4,128]{2,1,0:T(4,128)} %bitcast.13), calls=%async_computation.2 | async-start | bytes 131072 | tf_op jit(solution)/shard_map/all_to_all | solution.py:72
  56.5 192.4 %all-to-all-start.1 = ((f32[32,4,128,128]{3,2,1,0:T(8,128)}), f32[32,4,128,128]{3,2,1,0:T(8,128)}, u32[]{:S(2)}, u32[]{:S(2)}) async-start(f32[32,4,128,128]{3,2,1,0:T(8,128)} %bitcast.37), calls=%async_computation.1 | async-start | bytes 16777216 | tf_op jit(solution)/shard_map/all_to_all | solution.py:71
  65.9 275.2 %reduce-scatter.2.cloned.1.call-start = ((), (), s32[]{:S(2)}) async-start(), calls=%async_computation.4 | async-start | bytes 9437184 | tf_op jit(solution)/shard_map/reduce_scatter | solution.py:19
  271.0 7.5 %copy-start = (f32[64,128,1]{2,0,1:T(8,128)S(1)}, f32[64,128,1]{2,0,1:T(8,128)}, u32[]{:S(2)}) copy-start(f32[64,128,1]{2,0,1:T(8,128)} %copy.12) | copy-start | bytes 98308
Sparse Core Ops, SparseCore 0:
  282.8 58.2 reduce-scatter.1
where the time goes:
time: 396 us; the launch traced here: 391 us
  waiting for transfers between devices  242 us (61%)
  local copies, waits for them, and re-layouts  46.1 us (12%)
  blocking collectives  36.5 us (9%)
  starting transfers between devices  25.5 us (6%)
  other arithmetic  19.1 us (5%)
  between operations  14.2 us (4%)
  matrix products  7.67 us (2%)
    all_to_all x1, waiting for transfers between devices, local(): lax.all_to_all(send_vals, SHARD, split_axis=0, concat_axis=0, tiled=True)  177 us
    reduce_scatter x1, waiting for transfers between devices, sent_together(): lax.psum_scatter(both, axis, scatter_dimension=dim, tiled=True)  58.4 us
    psum x4, blocking collectives, one_axis_at_a_time(): value = lax.psum(value, axis)  36.5 us
    unnamed x3, local copies, waits for them, and re-layouts  13.1 us
    all_to_all x1, starting transfers between devices, local(): lax.all_to_all(send_ids, SHARD, split_axis=0, concat_axis=0, tiled=True)  12 us
    scatter x1, local copies, waits for them, and re-layouts, local(): jnp.zeros((nshard * CAP, rows, width), jnp.float32).at[slot_of].set(masked)  12 us
    all_to_all x1, starting transfers between devices, local(): lax.all_to_all(send_vals, SHARD, split_axis=0, concat_axis=0, tiled=True)  9.35 us
    dot_general x1, local copies, waits for them, and re-layouts, accumulate(): jnp.dot(onehot, values.reshape(slots, -1), precision=lax.Precision.HIGHES...  8.99 us
  transfers between devices with their start and end apart: 4, of which 3 were waited for; matrix products, arithmetic and copies ran while one was open for 8% of the time, Pallas kernels for 0%

commit v1 on v0

v1 whole, which is shorter than its diff:
```python
import math

import jax
import jax.numpy as jnp
from jax import lax
from jax.experimental import pallas as pl
from jax.experimental.pallas import tpu as pltpu
from jax.sharding import Mesh
from jax.sharding import PartitionSpec as P

NX, NC, NY, NZ = 4, 2, 4, 8
NP = NX * NC * NY
KB, BR, D = 64, 128, 128
BLK = 64
NG = BR // NP
K = NP * KB
CH = NY * BLK
PITCH = BR + 8
MESH = pl.DeviceIdType.MESH
REP = ("x", "c")
SHARD = ("y", "z")
LIMIT = 0.2 * math.sqrt(BLK * NY * NZ * BR * D)


def kernel(
    grads, meta, out,
    nat, xs, rv, mrv, kc, kt, oh, rhs, part, tpart, zr, tzr, ym, yrv, nv, n1, n2s, n2,
    lsem, p1s, p1r, msem, mrsem, zs, zrs, ys, yr, nsem,
):
    x, c, y, z = (lax.axis_index(a) for a in ("x", "c", "y", "z"))
    me = (x * NC + c) * NY + y

    def plane(e):
        px = lax.rem(x + e // (NC * NY), NX)
        pc = lax.rem(c + (e // NY) % NC, NC)
        py = lax.rem(y + e % NY, NY)
        return {"x": px, "c": pc, "y": py}, (px * NC + pc) * NY + py

    def zdev(d):
        return {"z": lax.rem(z + d, NZ)}

    def wait_bytes(ref, sem):
        pltpu.make_async_copy(ref, ref, sem).wait()

    def load(b, _):
        pltpu.make_async_copy(
            grads.at[pl.ds(b * BR, BR)], nat.at[pl.ds(pl.multiple_of(b * PITCH, 8), BR)], lsem
        ).start()
        return 0

    lax.fori_loop(0, KB, load, 0)

    barrier = pltpu.get_barrier_semaphore()

    def greet(e, _):
        pl.semaphore_signal(barrier, inc=1, device_id=plane(e)[0], device_id_type=MESH)
        return 0

    lax.fori_loop(1, NP, greet, 0)

    def greet_z(d, _):
        pl.semaphore_signal(barrier, inc=1, device_id=zdev(d), device_id_type=MESH)
        return 0

    lax.fori_loop(1, NZ, greet_z, 0)
    wait_bytes(nat.at[pl.ds(0, KB * BR)], lsem)

    def prep(g):
        def one(q, _):
            xs[g, q] = nat[pl.ds(q * NG + g, KB, stride=PITCH), :]
            return 0

        lax.fori_loop(0, NP, one, 0)
        rv[g, me] = xs[g, me]

    def send_p1(g):
        def one(i, _):
            dev, q = plane(lax.rem(i * 13 + 8 * g, NP))

            @pl.when(q != me)
            def _():
                pltpu.make_async_remote_copy(
                    src_ref=xs.at[g, q], dst_ref=rv.at[g, me], send_sem=p1s.at[g],
                    recv_sem=p1r.at[g], device_id=dev, device_id_type=MESH,
                ).start()

            return 0

        lax.fori_loop(0, NP, one, 0)

    def z_copy(src, dst, i, k, d):
        return pltpu.make_async_remote_copy(
            src_ref=src, dst_ref=dst, send_sem=zs.at[i, d, k], recv_sem=zrs.at[i, d, k],
            device_id=zdev(1 if d == 0 else NZ - 1), device_id_type=MESH,
        )

    def z_refs(p, r, k, d, half):
        t = 4 - k
        lo, n = (d * half, half) if k == 0 else (0, 2 * half)
        return p.at[t if d == 0 else (NZ - t) % NZ, pl.ds(lo, n)], r.at[d, k, pl.ds(lo, n)]

    def z_step(p, r, i, k, half):
        for d in range(2):
            if k > 0:
                src, dst = z_refs(p, r, k - 1, d, half)
                z_copy(src, dst, i, k - 1, d).wait_recv()
                own, _ = z_refs(p, r, k, d, half)
                if k == 1:
                    own = own.at[pl.ds(d * half, half)]
                own[...] += dst[...]
            src, dst = z_refs(p, r, k, d, half)
            z_copy(src, dst, i, k, d).start()

    def z_final(p, r, i, half):
        for d in range(2):
            src, dst = z_refs(p, r, 3, d, half)
            z_copy(src, dst, i, 3, d).wait_recv()
        return p[0] + r[0, 3] + r[1, 3]

    prep(0)
    pl.semaphore_wait(barrier, NP - 1 + NZ - 1)

    def send_meta(e, _):
        dev, q = plane(e)
        pltpu.make_async_remote_copy(
            src_ref=meta.at[q], dst_ref=mrv.at[me], send_sem=msem, recv_sem=mrsem,
            device_id=dev, device_id_type=MESH,
        ).start()
        return 0

    lax.fori_loop(1, NP, send_meta, 0)
    mrv[me] = meta[me]
    send_p1(0)
    for g in range(1, NG):
        prep(g)
        send_p1(g)

    wait_bytes(mrv.at[pl.ds(0, NP - 1)], mrsem)

    def keys(j, _):
        lane = lax.broadcasted_iota(jnp.int32, (8, 128), 1)
        tile = jnp.where(lane < KB, mrv[2 * j], pltpu.roll(mrv[2 * j + 1], KB, 1))
        row = lax.broadcasted_iota(jnp.int32, (8, 128), 0)
        rel = tile - z * CH
        rel = jnp.where(rel < 0, rel + NZ * CH, rel)
        tile = jnp.where(row == 0, rel, tile)
        kc[:, pl.ds(pl.multiple_of(j * 128, 128), 128)] = tile
        wide = jnp.concatenate([tile.astype(jnp.float32)] * 16, axis=0)
        kt[pl.ds(pl.multiple_of(j * 128, 128), 128), :] = wide.T
        return 0

    lax.fori_loop(0, NP // 2, keys, 0)

    def hot(m, _):
        at = pl.multiple_of(m * 32, 32)
        rows = lax.broadcasted_iota(jnp.int32, (32, K), 0) + at
        key = jnp.broadcast_to(kc[0:1, :], (32, K))
        oh[pl.ds(at, 32), :] = jnp.where(rows == key, 1.0, 0.0).astype(jnp.bfloat16)
        return 0

    lax.fori_loop(0, NZ * CH // 32, hot, 0)

    def total(t, _):
        tot = lax.dot_general(
            kc[...].astype(jnp.float32).astype(jnp.bfloat16), oh[pl.ds(pl.multiple_of(t * CH, CH), CH), :],
            (((1,), (1,)), ((), ())), preferred_element_type=jnp.float32,
        )
        tpart[t, 0:8] = tot[:, 0:128]
        tpart[t, 8:16] = tot[:, 128:256]
        return 0

    lax.fori_loop(0, NZ, total, 0)
    for k in range(4):
        z_step(tpart, tzr, NG, k, 8)
    tots = z_final(tpart, tzr, NG, 8)
    tpart[0] = 1.0 / jnp.maximum(tots, 1.0)

    def combine(g):
        wait_bytes(rv.at[g, pl.ds(0, NP - 1)], p1r.at[g])

        def split(j, _):
            at = pl.ds(pl.multiple_of(j * 128, 128), 128)
            v = rv[g, pl.ds(2 * j, 2)].reshape(128, D)
            v = jnp.where(kt[at, 1 + g : 2 + g] > 0.0, v, 0.0)
            hi = v.astype(jnp.bfloat16)
            rhs[at, 0:D] = hi
            rhs[at, D : 2 * D] = (v - hi.astype(jnp.float32)).astype(jnp.bfloat16)
            return 0

        lax.fori_loop(0, NP // 2, split, 0)

        def chunk(t, _):
            both = jnp.dot(
                oh[pl.ds(pl.multiple_of(t * CH, CH), CH), :], rhs[...],
                preferred_element_type=jnp.float32,
            )
            part[g, t] = both[:, 0:D] + both[:, D : 2 * D]
            return 0

        lax.fori_loop(0, NZ, chunk, 0)

    def finish(g):
        fin = z_final(part.at[g], zr.at[g], g, CH // 2)
        sq = jnp.zeros((8, D), jnp.float32)
        for h in range(2):
            inv = jnp.broadcast_to(tpart[0, 8 * h + 1 + g : 8 * h + 2 + g], (128, 128)).T
            mean = fin[128 * h : 128 * h + 128] * inv
            ym[g, 128 * h : 128 * h + 128] = mean
            sq = sq + jnp.sum((mean * mean).reshape(16, 8, D), axis=0)
        nv[...] = sq if g == 0 else nv[...] + sq

    def send_y(g):
        yrv[g, y] = ym[g, pl.ds(pl.multiple_of(y * BLK, BLK), BLK)]
        for dy in range(1, NY):
            py = lax.rem(y + dy, NY)
            pltpu.make_async_remote_copy(
                src_ref=ym.at[g, pl.ds(pl.multiple_of(py * BLK, BLK), BLK)], dst_ref=yrv.at[g, y],
                send_sem=ys.at[g], recv_sem=yr.at[g], device_id={"y": py}, device_id_type=MESH,
            ).start()

    def step(g, k):
        z_step(part.at[g], zr.at[g], g, k, CH // 2)

    for g in range(NG):
        combine(g)
        step(g, 0)
        if g > 0:
            step(g - 1, 3)
        step(g, 1)
        if g > 0:
            finish(g - 1)
            send_y(g - 1)
        step(g, 2)
    step(NG - 1, 3)
    finish(NG - 1)

    n1[me] = nv[...]

    def norm_plane(e, _):
        dev, _ = plane(e)
        pltpu.make_async_remote_copy(
            src_ref=nv, dst_ref=n1.at[me], send_sem=nsem.at[0], recv_sem=nsem.at[1],
            device_id=dev, device_id_type=MESH,
        ).start()
        return 0

    lax.fori_loop(1, NP, norm_plane, 0)
    send_y(NG - 1)
    wait_bytes(n1.at[pl.ds(0, NP - 1)], nsem.at[1])
    n2s[...] = jnp.sum(n1[...], axis=0)
    n2[z] = n2s[...]

    def norm_z(d, _):
        pltpu.make_async_remote_copy(
            src_ref=n2s, dst_ref=n2.at[z], send_sem=nsem.at[2],
            recv_sem=nsem.at[3], device_id=zdev(d), device_id_type=MESH,
        ).start()
        return 0

    lax.fori_loop(1, NZ, norm_z, 0)
    for g in range(NG):
        wait_bytes(yrv.at[g, pl.ds(0, NY - 1)], yr.at[g])
    wait_bytes(n2.at[pl.ds(0, NZ - 1)], nsem.at[3])
    norm2 = jnp.sum(jnp.sum(n2[...], axis=0), axis=(0, 1), keepdims=True)
    scale = jnp.minimum(1.0, LIMIT / jnp.sqrt(norm2 + 1e-06))
    for g in range(NG):
        for s in range(NY):
            out[pl.ds(s * NG + g, BLK, stride=NY * NG), :] = yrv[g, s] * scale

    wait_bytes(mrv.at[pl.ds(0, NP - 1)], msem)
    for g in range(NG):
        wait_bytes(xs.at[g, pl.ds(0, NP - 1)], p1s.at[g])
        wait_bytes(yrv.at[g, pl.ds(0, NY - 1)], ys.at[g])
    for i in range(NG + 1):
        for k in range(4):
            for d in range(2):
                p, r, half = (tpart, tzr, 8) if i == NG else (part.at[i], zr.at[i], CH // 2)
                z_copy(*z_refs(p, r, k, d, half), i, k, d).wait_send()
    wait_bytes(n1.at[pl.ds(0, NP - 1)], nsem.at[0])
    wait_bytes(n2.at[pl.ds(0, NZ - 1)], nsem.at[2])


def local(grads, counts, block_owner, block_local):
    owner = block_owner.reshape(KB)
    keys = (owner % NZ) * CH + (owner // NZ) * BLK + block_local.reshape(KB)
    rows = counts.reshape(KB, BR).T.reshape(NP, NG, KB)
    meta = jnp.concatenate(
        [jnp.broadcast_to(keys[None, None], (NP, 1, KB)), rows, jnp.zeros((NP, 7 - NG, KB), jnp.int32)],
        axis=1,
    )
    meta = jnp.pad(meta, ((0, 0), (0, 0), (0, 128 - KB)))
    f32 = jnp.float32
    vmem = pltpu.VMEM
    dma = pltpu.SemaphoreType.DMA
    out = pl.pallas_call(
        kernel,
        out_shape=jax.ShapeDtypeStruct((BLK * NY * NG, D), f32),
        in_specs=[pl.BlockSpec(memory_space=pl.ANY), pl.BlockSpec(memory_space=vmem)],
        out_specs=pl.BlockSpec(memory_space=vmem),
        scratch_shapes=[
            vmem((KB * PITCH, D), f32),
            vmem((NG, NP, KB, D), f32),
            vmem((NG, NP, KB, D), f32),
            vmem((NP, 8, 128), jnp.int32),
            vmem((8, K), jnp.int32),
            vmem((K, 128), f32),
            vmem((NZ * CH, K), jnp.bfloat16),
            vmem((K, 2 * D), jnp.bfloat16),
            vmem((NG, NZ, CH, D), f32),
            vmem((NZ, 16, 128), f32),
            vmem((NG, 2, 4, CH, D), f32),
            vmem((2, 4, 16, 128), f32),
            vmem((NG, CH, D), f32),
            vmem((NG, NY, BLK, D), f32),
            vmem((8, D), f32),
            vmem((NP, 8, D), f32),
            vmem((8, D), f32),
            vmem((NZ, 8, D), f32),
            dma,
            dma((NG,)),
            dma((NG,)),
            dma,
            dma,
            dma((NG + 1, 2, 4)),
            dma((NG + 1, 2, 4)),
            dma((NG,)),
            dma((NG,)),
            dma((4,)),
        ],
        compiler_params=pltpu.CompilerParams(
            collective_id=0, has_side_effects=True, vmem_limit_bytes=60 * 2**20
        ),
        name="table_mean",
    )(grads.reshape(KB * BR, D), meta)
    return out.reshape(BLK, NY * NG, D)


def solution(mesh):
    finer = Mesh(mesh.devices.reshape(NX, NC, NY, NZ), ("x", "c", "y", "z"))
    return jax.shard_map(
        local,
        mesh=finer,
        in_specs=(
            P(REP, SHARD, None, None, None),
            P(REP, SHARD, None, None),
            P(REP, SHARD, None, None),
            P(REP, SHARD, None),
        ),
        out_specs=P(SHARD, REP, None),
        check_vma=False,
    )
```

time: 396 us -> 119 us (0.30); the launches traced: 391 us -> 119 us
  waiting for transfers between devices: 242 us -> 0 us
  Pallas kernels: 0 us -> 114 us
  local copies, waits for them, and re-layouts: 46.1 us -> 3.47 us
  blocking collectives: 36.5 us -> 0 us
  starting transfers between devices: 25.5 us -> 0 us
  other arithmetic: 19.1 us -> 0.76 us
  between operations: 14.2 us -> 0.04 us
  matrix products: 7.67 us -> 0 us
    all_to_all x3 -> x0, waiting for transfers between devices: 183 us -> none  [the longest x1 177 us: local(): lax.all_to_all(send_vals, SHARD, split_axis=0, concat_axis=0, tiled=True)]
    pallas_call x0 -> x1, Pallas kernels: none -> 114 us  [local(): pl.pallas_call(kernel, out_shape=jax.ShapeDtypeStruct((BLK * NY * NG, D),...]
    reduce_scatter x1 -> x0, waiting for transfers between devices: 58.4 us -> none  [sent_together(): lax.psum_scatter(both, axis, scatter_dimension=dim, tiled=True)]
    psum x4 -> x0, blocking collectives: 36.5 us -> none  [one_axis_at_a_time(): value = lax.psum(value, axis)]
    all_to_all x3 -> x0, starting transfers between devices: 25.2 us -> none  [the longest x1 12 us: local(): lax.all_to_all(send_ids, SHARD, split_axis=0, concat_axis=0, tiled=True)]
    scatter x2 -> x0, local copies, waits for them, and re-layouts: 12.9 us -> none  [the longest x1 12 us: local(): jnp.zeros((nshard * CAP, rows, width), jnp.float32).at[slot_of].set(masked)]
    unnamed x3 -> x1, local copies, waits for them, and re-layouts: 13.1 us -> 1.87 us
    dot_general x1 -> x0, local copies, waits for them, and re-layouts: 8.99 us -> none  [accumulate(): jnp.dot(onehot, values.reshape(slots, -1), precision=lax.Precision.HIGHES...]
  transfers between devices with their start and end apart: 4 -> 0, of which waited for: 3 -> 0; matrix products, arithmetic and copies ran while one was open for 8% -> 0% of each run, Pallas kernels for 0% -> 0%
where the time goes in v1:
time: 119 us
  Pallas kernels  114 us (96%)
  local copies, waits for them, and re-layouts  3.47 us (3%)
    pallas_call x1, Pallas kernels, local(): pl.pallas_call(kernel, out_shape=jax.ShapeDtypeStruct((BLK * NY * NG, D),...  114 us

profile of v1, /device:TPU:1, one launch (start us, length us, event | category | flops | bytes accessed | tf_op | source)
XLA Modules:
  0.0 118.6 jit_solution(10997335581763160640)
XLA Ops:
  0.0 0.7 fusion.3
  0.7 0.1 pad.7.clone
  0.8 0.8 copy.5
  1.6 0.1 add_add_fusion
  1.7 0.7 pad.4.meta
  2.4 114.3 %table_mean.1 = f32[1024,128]{1,0:T(8,128)} custom-call(f32[8192,128]{1,0:T(8,128)} %bitcast.23, s32[32,8,128]{2,1,0:T(8,128)} %pad.4.meta), custom_call_target="tpu_custom_call" | custom-call | tf_op jit(solution)/shard_map/table_mean/pallas_call | solution.py:295
  116.7 1.9 %copy.7 = f32[64,16,128]{2,1,0:T(8,128)} copy(f32[64,16,128]{2,1,0:T(8,128)} %bitcast.24) | data formatting | bytes 1048576
  (2 shorter events, 0.0 us)

commit v2 on v1

v2 whole, which is shorter than its diff:
```python
import math

import jax
import jax.numpy as jnp
from jax import lax
from jax.experimental import pallas as pl
from jax.experimental.pallas import tpu as pltpu
from jax.sharding import Mesh
from jax.sharding import PartitionSpec as P

NX, NC, NY, NZ = 4, 2, 4, 8
NP = NX * NC * NY
KB, BR, D = 64, 128, 128
BLK = 64
NG = BR // NP
K = NP * KB
CH = NY * BLK
PITCH = BR + 8
POS = (7, 5, 3, 1, 0, 2, 4, 6)
FIRST = 3
MESH = pl.DeviceIdType.MESH
REP = ("x", "c")
SHARD = ("y", "z")
LIMIT = 0.2 * math.sqrt(BLK * NY * NZ * BR * D)


def kernel(
    grads, counts, owner, ids, out,
    nat, cv, ov, iv, meta, xs, rv, mrv, kc, kt, oh, rhs, part, tpart, zr, tzr, ym, yrv, nv, n1, n2s, n2,
    lsem, csem, p1s, p1r, msem, mrsem, zs, zrs, ys, yr, nsem,
):
    x, c, y, z = (lax.axis_index(a) for a in ("x", "c", "y", "z"))
    me = (x * NC + c) * NY + y
    px = [lax.rem(x + d, NX) for d in range(NX)]
    pc = [c, 1 - c]
    py = [lax.rem(y + d, NY) for d in range(NY)]

    def plane(e):
        dx, dc, dy = e // (NC * NY), (e // NY) % NC, e % NY
        return {"x": px[dx], "c": pc[dc], "y": py[dy]}, (px[dx] * NC + pc[dc]) * NY + py[dy]

    def zdev(d):
        return {"z": lax.rem(z + d, NZ)}

    def wait_bytes(ref, sem):
        pltpu.make_async_copy(ref, ref, sem).wait()

    small = [
        pltpu.make_async_copy(s, d, csem.at[i])
        for i, (s, d) in enumerate(((counts, cv), (owner, ov), (ids, iv)))
    ]
    for cp in small:
        cp.start()

    def load(b, _):
        pltpu.make_async_copy(
            grads.at[pl.ds(pl.multiple_of(b * BR, 8), BR)],
            nat.at[pl.ds(pl.multiple_of(b * PITCH, 8), BR)], lsem,
        ).start()
        return 0

    barrier = pltpu.get_barrier_semaphore()
    for e in range(1, NP):
        pl.semaphore_signal(barrier, inc=1, device_id=plane(e)[0], device_id_type=MESH)
    for d in range(1, NZ):
        pl.semaphore_signal(barrier, inc=1, device_id=zdev(d), device_id_type=MESH)
    lax.fori_loop(0, KB, load, 0, unroll=8)

    for cp in small:
        cp.wait()
    o = ov[...]
    key = ((o & (NZ - 1)) * CH + (o >> 3) * BLK + iv[...]).astype(jnp.float32)
    key = jnp.broadcast_to(jnp.concatenate([key, key], axis=1), (8, 128))
    cf = cv[...].astype(jnp.float32)
    ct = jnp.concatenate([cf, cf], axis=0).T
    low = lax.broadcasted_iota(jnp.int32, (8, 128), 0) < NG
    for j in range(NP // 2):
        two = ct[8 * j : 8 * j + 8]
        meta[2 * j] = jnp.where(low, two, key)
        meta[2 * j + 1] = jnp.where(low, pltpu.roll(two, NG, 0), key)

    def prep(g):
        def one(q, _):
            xs[g, q] = nat[pl.ds(q * NG + g, KB, stride=PITCH), :]
            return 0

        lax.fori_loop(0, NP, one, 0, unroll=4)
        rv[g, me] = xs[g, me]

    def send_plane(e, src, dst, send, recv):
        dev, q = plane(e)
        pltpu.make_async_remote_copy(
            src_ref=src.at[q] if src is not nv else src, dst_ref=dst.at[me], send_sem=send, recv_sem=recv,
            device_id=dev, device_id_type=MESH,
        ).start()

    def send_p1(g):
        for i in range(NP):
            e = (i * 13 + 8 * g) % NP
            if e:
                send_plane(e, xs.at[g], rv.at[g], p1s.at[g], p1r.at[g])

    def z_copy(src, dst, i, k, d, u):
        return pltpu.make_async_remote_copy(
            src_ref=src, dst_ref=dst, send_sem=zs.at[i, d, u, k], recv_sem=zrs.at[i, d, u, k],
            device_id=zdev(1 if d == 0 else NZ - 1), device_id_type=MESH,
        )

    def z_refs(p, r, k, d, u, half):
        t = 4 - k if d == 0 else 4 + k
        return p.at[POS[t % NZ], pl.ds(u * half, half)], r.at[d, u, k]

    def z_step(p, r, i, j, half):
        for far in (1, 0):
            for d in range(2):
                u = d if far else 1 - d
                k = j if far else j + 1
                if k > 3:
                    continue
                own, slot = z_refs(p, r, k, d, u, half)
                if j > 0:
                    src, dst = z_refs(p, r, k - 1, d, u, half)
                    z_copy(src, dst, i, k - 1, d, u).wait_recv()
                    own[...] += dst[...]
                z_copy(own, slot, i, k, d, u).start()

    def z_final(p, r, i, u, half):
        for d in range(2):
            src, dst = z_refs(p, r, 3, d, u, half)
            z_copy(src, dst, i, 3, d, u).wait_recv()
        return p[POS[0], u * half : u * half + half] + r[0, u, 3] + r[1, u, 3]

    pl.semaphore_wait(barrier, NP - 1 + NZ - 1)
    for e in range(1, NP):
        send_plane(e, meta, mrv, msem, mrsem)
    mrv[me] = meta[me]
    wait_bytes(nat.at[pl.ds(0, KB * BR)], lsem)
    for g in range(NG):
        prep(g)
        send_p1(g)

    wait_bytes(mrv.at[pl.ds(0, NP - 1)], mrsem)

    def keys(j, _):
        lane = lax.broadcasted_iota(jnp.int32, (8, 128), 1)
        tile = jnp.where(lane < KB, mrv[2 * j], mrv[2 * j + 1])
        row = lax.broadcasted_iota(jnp.int32, (8, 128), 0)
        at = tile.astype(jnp.int32)
        t = (at >> 8) - z
        t = jnp.where(t < 0, t + NZ, t)
        t = jnp.where(t < 4, 7 - 2 * t, 2 * t - 8)
        tile = jnp.where(row < NG, tile, (t * CH + (at & (CH - 1))).astype(jnp.float32))
        kc[:, pl.ds(pl.multiple_of(j * 128, 128), 128)] = tile
        wide = jnp.concatenate([tile] * 16, axis=0)
        kt[pl.ds(pl.multiple_of(j * 128, 128), 128), :] = wide.T
        return 0

    lax.fori_loop(0, NP // 2, keys, 0, unroll=2)

    def hot(m, _):
        at = pl.multiple_of(m * 32, 32)
        rows = lax.broadcasted_iota(jnp.int32, (32, K), 0) + at
        key = jnp.broadcast_to(kc[NG : NG + 1, :].astype(jnp.int32), (32, K))
        oh[pl.ds(at, 32), :] = jnp.where(rows == key, 1.0, 0.0).astype(jnp.bfloat16)
        return 0

    lax.fori_loop(0, NZ * CH // 32, hot, 0)

    def total(t, _):
        tot = lax.dot_general(
            kc[...].astype(jnp.bfloat16), oh[pl.ds(pl.multiple_of(t * CH, CH), CH), :],
            (((1,), (1,)), ((), ())), preferred_element_type=jnp.float32,
        )
        tpart[t, 0:8] = tot[:, 0:128]
        tpart[t, 8:16] = tot[:, 128:256]
        return 0

    lax.fori_loop(0, NZ, total, 0)

    def split(g):
        wait_bytes(rv.at[g, pl.ds(0, NP - 1)], p1r.at[g])

        def one(j, _):
            at = pl.ds(pl.multiple_of(j * 128, 128), 128)
            v = rv[g, pl.ds(2 * j, 2)].reshape(128, D)
            v = jnp.where(kt[at, g : g + 1] > 0.0, v, 0.0)
            hi = v.astype(jnp.bfloat16)
            rhs[at, 0:D] = hi
            rhs[at, D : 2 * D] = (v - hi.astype(jnp.float32)).astype(jnp.bfloat16)
            return 0

        lax.fori_loop(0, NP // 2, one, 0, unroll=4)

    def combine(g, lo, n):
        both = jnp.dot(oh[lo * CH : (lo + n) * CH, :], rhs[...], preferred_element_type=jnp.float32)
        part[g, lo : lo + n] = (both[:, 0:D] + both[:, D : 2 * D]).reshape(n, CH, D)

    def finish(g):
        sq = jnp.zeros((8, D), jnp.float32)
        for h in range(2):
            fin = z_final(part.at[g], zr.at[g], g, h, CH // 2)
            inv = jnp.broadcast_to(tpart[POS[0], 8 * h + g : 8 * h + g + 1], (128, 128)).T
            mean = fin * inv
            ym[g, 128 * h : 128 * h + 128] = mean
            sq = sq + jnp.sum((mean * mean).reshape(16, 8, D), axis=0)
        nv[...] = sq if g == 0 else nv[...] + sq

    def send_y(g):
        yrv[g, y] = ym[g, pl.ds(pl.multiple_of(y * BLK, BLK), BLK)]
        for dy in range(1, NY):
            pltpu.make_async_remote_copy(
                src_ref=ym.at[g, pl.ds(pl.multiple_of(py[dy] * BLK, BLK), BLK)], dst_ref=yrv.at[g, y],
                send_sem=ys.at[g], recv_sem=yr.at[g], device_id={"y": py[dy]}, device_id_type=MESH,
            ).start()

    def step(g, j):
        z_step(part.at[g], zr.at[g], g, j, CH // 2)

    z_step(tpart, tzr, NG, 0, 8)
    for g in range(NG):
        split(g)
        combine(g, 0, FIRST)
        step(g, 0)
        if g == 0:
            z_step(tpart, tzr, NG, 1, 8)
        combine(g, FIRST, NZ - FIRST)
        if g > 0:
            finish(g - 1)
            send_y(g - 1)
        for j in range(1, 4):
            step(g, j)
            if g == 0 and j < 3:
                z_step(tpart, tzr, NG, j + 1, 8)
        if g == 0:
            for u in range(2):
                tots = z_final(tpart, tzr, NG, u, 8)
                tpart[POS[0], 8 * u : 8 * u + 8] = 1.0 / jnp.maximum(tots, 1.0)
    finish(NG - 1)

    for e in range(1, NP):
        send_plane(e, nv, n1, nsem.at[0], nsem.at[1])
    n1[me] = nv[...]
    send_y(NG - 1)
    wait_bytes(n1.at[pl.ds(0, NP - 1)], nsem.at[1])
    n2s[...] = jnp.sum(n1[...], axis=0)
    for d in range(1, NZ):
        pltpu.make_async_remote_copy(
            src_ref=n2s, dst_ref=n2.at[z], send_sem=nsem.at[2], recv_sem=nsem.at[3],
            device_id=zdev(d), device_id_type=MESH,
        ).start()
    n2[z] = n2s[...]
    for g in range(NG):
        wait_bytes(yrv.at[g, pl.ds(0, NY - 1)], yr.at[g])
    wait_bytes(n2.at[pl.ds(0, NZ - 1)], nsem.at[3])
    norm2 = jnp.sum(jnp.sum(n2[...], axis=0), axis=(0, 1), keepdims=True)
    scale = jnp.minimum(1.0, LIMIT / jnp.sqrt(norm2 + 1e-06))
    for g in range(NG):
        for s in range(NY):
            out[pl.ds(s * NG + g, BLK, stride=NY * NG), :] = yrv[g, s] * scale

    wait_bytes(mrv.at[pl.ds(0, NP - 1)], msem)
    for g in range(NG):
        wait_bytes(xs.at[g, pl.ds(0, NP - 1)], p1s.at[g])
        wait_bytes(yrv.at[g, pl.ds(0, NY - 1)], ys.at[g])
    for i in range(NG + 1):
        p, r, half = (tpart, tzr, 8) if i == NG else (part.at[i], zr.at[i], CH // 2)
        for d in range(2):
            for u in range(2):
                for k in range(0 if u == d else 1, 4):
                    z_copy(*z_refs(p, r, k, d, u, half), i, k, d, u).wait_send()
    wait_bytes(n1.at[pl.ds(0, NP - 1)], nsem.at[0])
    wait_bytes(n2.at[pl.ds(0, NZ - 1)], nsem.at[2])


def local(grads, counts, block_owner, block_local):
    f32 = jnp.float32
    i32 = jnp.int32
    vmem = pltpu.VMEM
    dma = pltpu.SemaphoreType.DMA
    out = pl.pallas_call(
        kernel,
        out_shape=jax.ShapeDtypeStruct((BLK * NY * NG, D), f32),
        in_specs=[pl.BlockSpec(memory_space=pl.ANY)] * 4,
        out_specs=pl.BlockSpec(memory_space=vmem),
        scratch_shapes=[
            vmem((KB * PITCH, D), f32),
            vmem((KB, BR), i32),
            vmem((1, KB), i32),
            vmem((1, KB), i32),
            vmem((NP, 8, 128), f32),
            vmem((NG, NP, KB, D), f32),
            vmem((NG, NP, KB, D), f32),
            vmem((NP, 8, 128), f32),
            vmem((8, K), f32),
            vmem((K, 128), f32),
            vmem((NZ * CH, K), jnp.bfloat16),
            vmem((K, 2 * D), jnp.bfloat16),
            vmem((NG, NZ, CH, D), f32),
            vmem((NZ, 16, 128), f32),
            vmem((NG, 2, 2, 4, CH // 2, D), f32),
            vmem((2, 2, 4, 8, 128), f32),
            vmem((NG, CH, D), f32),
            vmem((NG, NY, BLK, D), f32),
            vmem((8, D), f32),
            vmem((NP, 8, D), f32),
            vmem((8, D), f32),
            vmem((NZ, 8, D), f32),
            dma,
            dma((3,)),
            dma((NG,)),
            dma((NG,)),
            dma,
            dma,
            dma((NG + 1, 2, 2, 4)),
            dma((NG + 1, 2, 2, 4)),
            dma((NG,)),
            dma((NG,)),
            dma((4,)),
        ],
        compiler_params=pltpu.CompilerParams(
            collective_id=0, has_side_effects=True, vmem_limit_bytes=60 * 2**20
        ),
        name="table_mean",
    )(
        grads.reshape(KB * BR, D),
        counts.reshape(KB, BR),
        block_owner.reshape(1, KB),
        block_local.reshape(1, KB),
    )
    return out.reshape(BLK, NY * NG, D)


def solution(mesh):
    finer = Mesh(mesh.devices.reshape(NX, NC, NY, NZ), ("x", "c", "y", "z"))
    return jax.shard_map(
        local,
        mesh=finer,
        in_specs=(
            P(REP, SHARD, None, None, None),
            P(REP, SHARD, None, None),
            P(REP, SHARD, None, None),
            P(REP, SHARD, None),
        ),
        out_specs=P(SHARD, REP, None),
        check_vma=False,
    )
```

time: 119 us -> 104 us (0.87)
  Pallas kernels: 114 us -> 102 us
  local copies, waits for them, and re-layouts: 3.47 us -> 1.87 us
    pallas_call x1, Pallas kernels: 114 us -> 102 us  [local(): pl.pallas_call(kernel, out_shape=jax.ShapeDtypeStruct((BLK * NY * NG, D),...]
where the time goes in v2:
time: 104 us; the launch traced here: 103 us
  Pallas kernels  102 us (98%)
  local copies, waits for them, and re-layouts  1.87 us (2%)
    pallas_call x1, Pallas kernels, local(): pl.pallas_call(kernel, out_shape=jax.ShapeDtypeStruct((BLK * NY * NG, D),...  102 us

profile of v2, /device:TPU:1, one launch (start us, length us, event | category | flops | bytes accessed | tf_op | source)
XLA Modules:
  0.0 103.4 jit_solution(6034536248146538124)
XLA Ops:
  0.0 101.5 %table_mean.1 = f32[1024,128]{1,0:T(8,128)} custom-call(f32[8192,128]{1,0:T(8,128)} %bitcast.5, s32[64,128]{1,0:T(8,128)} %bitcast.7, s32[1,64]{1,0:T(1,128)} %bitcast.8, s32[1,64]{1,0:T(1,128)} %bitcast.9), custom_call_target="tpu_custom_call" | custom-call | tf_op jit(solution)/shard_map/table_mean/pallas_call | solution.py:280
  101.5 1.9 %copy.6 = f32[64,16,128]{2,1,0:T(8,128)} copy(f32[64,16,128]{2,1,0:T(8,128)} %bitcast.6) | data formatting | bytes 1048576

commit v3 on v2

--- a/solution.py
+++ b/solution.py
@@ -18,6 +18,7 @@
 PITCH = BR + 8
 POS = (7, 5, 3, 1, 0, 2, 4, 6)
 FIRST = 3
+SUB = 2
 MESH = pl.DeviceIdType.MESH
 REP = ("x", "c")
 SHARD = ("y", "z")
@@ -59,12 +60,12 @@
         ).start()
         return 0
 
+    lax.fori_loop(0, KB, load, 0, unroll=8)
     barrier = pltpu.get_barrier_semaphore()
     for e in range(1, NP):
         pl.semaphore_signal(barrier, inc=1, device_id=plane(e)[0], device_id_type=MESH)
     for d in range(1, NZ):
         pl.semaphore_signal(barrier, inc=1, device_id=zdev(d), device_id_type=MESH)
-    lax.fori_loop(0, KB, load, 0, unroll=8)
 
     for cp in small:
         cp.wait()
@@ -106,36 +107,46 @@
             device_id=zdev(1 if d == 0 else NZ - 1), device_id_type=MESH,
         )
 
-    def z_refs(p, r, k, d, u, half):
+    def z_refs(p, r, k, d, u, n):
         t = 4 - k if d == 0 else 4 + k
-        return p.at[POS[t % NZ], pl.ds(u * half, half)], r.at[d, u, k]
-
-    def z_step(p, r, i, j, half):
-        for far in (1, 0):
-            for d in range(2):
-                u = d if far else 1 - d
-                k = j if far else j + 1
-                if k > 3:
-                    continue
-                own, slot = z_refs(p, r, k, d, u, half)
-                if j > 0:
-                    src, dst = z_refs(p, r, k - 1, d, u, half)
-                    z_copy(src, dst, i, k - 1, d, u).wait_recv()
-                    own[...] += dst[...]
-                z_copy(own, slot, i, k, d, u).start()
-
-    def z_final(p, r, i, u, half):
+        return p.at[POS[t % NZ], pl.ds(u * n, n)], r.at[d, u, k]
+
+    def far(d, u, n):
+        return (u * 2 * n < rows_of(n)) == (d == 0)
+
+    def rows_of(n):
+        return 16 if n == 8 else CH
+
+    def z_step(p, r, i, j, n):
+        parts = rows_of(n) // n
+        for first in (True, False):
+            for v in range(parts // 2):
+                for d in range(2):
+                    u = v if (d == 0) == first else parts // 2 + v
+                    k = j if first else j + 1
+                    if k > 3:
+                        continue
+                    own, slot = z_refs(p, r, k, d, u, n)
+                    if j > 0:
+                        src, dst = z_refs(p, r, k - 1, d, u, n)
+                        z_copy(src, dst, i, k - 1, d, u).wait_recv()
+                        own[...] += dst[...]
+                    z_copy(own, slot, i, k, d, u).start()
+
+    def z_final(p, r, i, u, n):
         for d in range(2):
-            src, dst = z_refs(p, r, 3, d, u, half)
+            src, dst = z_refs(p, r, 3, d, u, n)
             z_copy(src, dst, i, 3, d, u).wait_recv()
-        return p[POS[0], u * half : u * half + half] + r[0, u, 3] + r[1, u, 3]
-
+        return p[POS[0], u * n : u * n + n] + r[0, u, 3] + r[1, u, 3]
+
+    wait_bytes(nat.at[pl.ds(0, KB * BR)], lsem)
+    prep(0)
     pl.semaphore_wait(barrier, NP - 1 + NZ - 1)
     for e in range(1, NP):
         send_plane(e, meta, mrv, msem, mrsem)
+    send_p1(0)
     mrv[me] = meta[me]
-    wait_bytes(nat.at[pl.ds(0, KB * BR)], lsem)
-    for g in range(NG):
+    for g in range(1, NG):
         prep(g)
         send_p1(g)
 
@@ -196,13 +207,17 @@
         part[g, lo : lo + n] = (both[:, 0:D] + both[:, D : 2 * D]).reshape(n, CH, D)
 
     def finish(g):
+        n = CH // SUB
         sq = jnp.zeros((8, D), jnp.float32)
-        for h in range(2):
-            fin = z_final(part.at[g], zr.at[g], g, h, CH // 2)
-            inv = jnp.broadcast_to(tpart[POS[0], 8 * h + g : 8 * h + g + 1], (128, 128)).T
-            mean = fin * inv
-            ym[g, 128 * h : 128 * h + 128] = mean
-            sq = sq + jnp.sum((mean * mean).reshape(16, 8, D), axis=0)
+        inv = [
+            jnp.broadcast_to(tpart[POS[0], 8 * h + g : 8 * h + g + 1], (128, 128)).T for h in range(2)
+        ]
+        for v in range(SUB // 2):
+            for u in (v, SUB // 2 + v):
+                fin = z_final(part.at[g], zr.at[g], g, u, n)
+                mean = fin * inv[u * n // 128][u * n % 128 : u * n % 128 + n]
+                ym[g, u * n : u * n + n] = mean
+                sq = sq + jnp.sum((mean * mean).reshape(n // 8, 8, D), axis=0)
         nv[...] = sq if g == 0 else nv[...] + sq
 
     def send_y(g):
@@ -214,7 +229,7 @@
             ).start()
 
     def step(g, j):
-        z_step(part.at[g], zr.at[g], g, j, CH // 2)
+        z_step(part.at[g], zr.at[g], g, j, CH // SUB)
 
     z_step(tpart, tzr, NG, 0, 8)
     for g in range(NG):
@@ -225,16 +240,21 @@
             z_step(tpart, tzr, NG, 1, 8)
         combine(g, FIRST, NZ - FIRST)
         if g > 0:
-            finish(g - 1)
-            send_y(g - 1)
-        for j in range(1, 4):
-            step(g, j)
-            if g == 0 and j < 3:
-                z_step(tpart, tzr, NG, j + 1, 8)
+            step(g - 1, 3)
+        step(g, 1)
         if g == 0:
+            z_step(tpart, tzr, NG, 2, 8)
+        if g == 1:
             for u in range(2):
                 tots = z_final(tpart, tzr, NG, u, 8)
                 tpart[POS[0], 8 * u : 8 * u + 8] = 1.0 / jnp.maximum(tots, 1.0)
+        if g > 0:
+            finish(g - 1)
+            send_y(g - 1)
+        step(g, 2)
+        if g == 0:
+            z_step(tpart, tzr, NG, 3, 8)
+    step(NG - 1, 3)
     finish(NG - 1)
 
     for e in range(1, NP):
@@ -263,11 +283,11 @@
         wait_bytes(xs.at[g, pl.ds(0, NP - 1)], p1s.at[g])
         wait_bytes(yrv.at[g, pl.ds(0, NY - 1)], ys.at[g])
     for i in range(NG + 1):
-        p, r, half = (tpart, tzr, 8) if i == NG else (part.at[i], zr.at[i], CH // 2)
+        p, r, n = (tpart, tzr, 8) if i == NG else (part.at[i], zr.at[i], CH // SUB)
         for d in range(2):
-            for u in range(2):
-                for k in range(0 if u == d else 1, 4):
-                    z_copy(*z_refs(p, r, k, d, u, half), i, k, d, u).wait_send()
+            for u in range(rows_of(n) // n):
+                for k in range(0 if far(d, u, n) else 1, 4):
+                    z_copy(*z_refs(p, r, k, d, u, n), i, k, d, u).wait_send()
     wait_bytes(n1.at[pl.ds(0, NP - 1)], nsem.at[0])
     wait_bytes(n2.at[pl.ds(0, NZ - 1)], nsem.at[2])
 
@@ -297,7 +317,7 @@
             vmem((K, 2 * D), jnp.bfloat16),
             vmem((NG, NZ, CH, D), f32),
             vmem((NZ, 16, 128), f32),
-            vmem((NG, 2, 2, 4, CH // 2, D), f32),
+            vmem((NG, 2, SUB, 4, CH // SUB, D), f32),
             vmem((2, 2, 4, 8, 128), f32),
             vmem((NG, CH, D), f32),
             vmem((NG, NY, BLK, D), f32),
@@ -311,8 +331,8 @@
             dma((NG,)),
             dma,
             dma,
-            dma((NG + 1, 2, 2, 4)),
-            dma((NG + 1, 2, 2, 4)),
+            dma((NG + 1, 2, SUB, 4)),
+            dma((NG + 1, 2, SUB, 4)),
             dma((NG,)),
             dma((NG,)),
             dma((4,)),

time: 104 us -> 96.8 us (0.931)
  Pallas kernels: 102 us -> 94.8 us
    pallas_call x1, Pallas kernels: 102 us -> 94.8 us  [local(): pl.pallas_call(kernel, out_shape=jax.ShapeDtypeStruct((BLK * NY * NG, D),...]
where the time goes in v3:
time: 96.8 us; the launch traced here: 96.6 us
  Pallas kernels  94.8 us (98%)
  local copies, waits for them, and re-layouts  1.87 us (2%)
    pallas_call x1, Pallas kernels, local(): pl.pallas_call(kernel, out_shape=jax.ShapeDtypeStruct((BLK * NY * NG, D),...  94.8 us

profile of v3, /device:TPU:1, one launch (start us, length us, event | category | flops | bytes accessed | tf_op | source)
XLA Modules:
  0.0 96.6 jit_solution(15431926327304301551)
XLA Ops:
  0.0 94.8 %table_mean.1 = f32[1024,128]{1,0:T(8,128)} custom-call(f32[8192,128]{1,0:T(8,128)} %bitcast.5, s32[64,128]{1,0:T(8,128)} %bitcast.7, s32[1,64]{1,0:T(1,128)} %bitcast.8, s32[1,64]{1,0:T(1,128)} %bitcast.9), custom_call_target="tpu_custom_call" | custom-call | tf_op jit(solution)/shard_map/table_mean/pallas_call | solution.py:300
  94.8 1.9 %copy.6 = f32[64,16,128]{2,1,0:T(8,128)} copy(f32[64,16,128]{2,1,0:T(8,128)} %bitcast.6) | data formatting | bytes 1048576

commit v4 on v3

--- a/solution.py
+++ b/solution.py
@@ -26,9 +26,9 @@
 
 
 def kernel(
-    grads, counts, owner, ids, out,
-    nat, cv, ov, iv, meta, xs, rv, mrv, kc, kt, oh, rhs, part, tpart, zr, tzr, ym, yrv, nv, n1, n2s, n2,
-    lsem, csem, p1s, p1r, msem, mrsem, zs, zrs, ys, yr, nsem,
+    grads, counts, owner, ids, out, scale,
+    nat, cv, ov, iv, meta, xs, rv, mrv, kc, kt, oh, rhs, part, tpart, zr, tzr, ym, yrv, rows, nv, n1, n2s, n2,
+    lsem, csem, p1s, p1r, msem, mrsem, zs, zrs, ys, yr, nsem, osem,
 ):
     x, c, y, z = (lax.axis_index(a) for a in ("x", "c", "y", "z"))
     me = (x * NC + c) * NY + y
@@ -100,6 +100,9 @@
             e = (i * 13 + 8 * g) % NP
             if e:
                 send_plane(e, xs.at[g], rv.at[g], p1s.at[g], p1r.at[g])
+            if g == 0 and i == 6:
+                for f in range(1, NP):
+                    send_plane(f, meta, mrv, msem, mrsem)
 
     def z_copy(src, dst, i, k, d, u):
         return pltpu.make_async_remote_copy(
@@ -142,8 +145,6 @@
     wait_bytes(nat.at[pl.ds(0, KB * BR)], lsem)
     prep(0)
     pl.semaphore_wait(barrier, NP - 1 + NZ - 1)
-    for e in range(1, NP):
-        send_plane(e, meta, mrv, msem, mrsem)
     send_p1(0)
     mrv[me] = meta[me]
     for g in range(1, NG):
@@ -271,12 +272,14 @@
     n2[z] = n2s[...]
     for g in range(NG):
         wait_bytes(yrv.at[g, pl.ds(0, NY - 1)], yr.at[g])
+        for s in range(NY):
+            rows[pl.ds(s * NG + g, BLK, stride=NY * NG), :] = yrv[g, s]
+    leave = pltpu.make_async_copy(rows, out, osem)
+    leave.start()
     wait_bytes(n2.at[pl.ds(0, NZ - 1)], nsem.at[3])
     norm2 = jnp.sum(jnp.sum(n2[...], axis=0), axis=(0, 1), keepdims=True)
-    scale = jnp.minimum(1.0, LIMIT / jnp.sqrt(norm2 + 1e-06))
-    for g in range(NG):
-        for s in range(NY):
-            out[pl.ds(s * NG + g, BLK, stride=NY * NG), :] = yrv[g, s] * scale
+    scale[...] = jnp.broadcast_to(jnp.minimum(1.0, LIMIT / jnp.sqrt(norm2 + 1e-06)), (8, D))
+    leave.wait()
 
     wait_bytes(mrv.at[pl.ds(0, NP - 1)], msem)
     for g in range(NG):
@@ -297,11 +300,14 @@
     i32 = jnp.int32
     vmem = pltpu.VMEM
     dma = pltpu.SemaphoreType.DMA
-    out = pl.pallas_call(
+    mean, scale = pl.pallas_call(
         kernel,
-        out_shape=jax.ShapeDtypeStruct((BLK * NY * NG, D), f32),
+        out_shape=(
+            jax.ShapeDtypeStruct((BLK * NY * NG, D), f32),
+            jax.ShapeDtypeStruct((8, D), f32),
+        ),
         in_specs=[pl.BlockSpec(memory_space=pl.ANY)] * 4,
-        out_specs=pl.BlockSpec(memory_space=vmem),
+        out_specs=(pl.BlockSpec(memory_space=pl.ANY), pl.BlockSpec(memory_space=vmem)),
         scratch_shapes=[
             vmem((KB * PITCH, D), f32),
             vmem((KB, BR), i32),
@@ -321,6 +327,7 @@
             vmem((2, 2, 4, 8, 128), f32),
             vmem((NG, CH, D), f32),
             vmem((NG, NY, BLK, D), f32),
+            vmem((BLK * NY * NG, D), f32),
             vmem((8, D), f32),
             vmem((NP, 8, D), f32),
             vmem((8, D), f32),
@@ -336,9 +343,10 @@
             dma((NG,)),
             dma((NG,)),
             dma((4,)),
+            dma,
         ],
         compiler_params=pltpu.CompilerParams(
-            collective_id=0, has_side_effects=True, vmem_limit_bytes=60 * 2**20
+            collective_id=0, has_side_effects=True, vmem_limit_bytes=52 * 2**20
         ),
         name="table_mean",
     )(
@@ -347,7 +355,7 @@
         block_owner.reshape(1, KB),
         block_local.reshape(1, KB),
     )
-    return out.reshape(BLK, NY * NG, D)
+    return (mean.reshape(BLK, 2, 8, D) * scale).reshape(BLK, NY * NG, D)
 
 
 def solution(mesh):

time: 96.8 us -> 96.1 us (level)
  Pallas kernels: 94.8 us -> 93 us
    pallas_call x1, Pallas kernels: 94.8 us -> 93 us  [local(): pl.pallas_call(kernel, out_shape=(jax.ShapeDtypeStruct((BLK * NY * NG, D)...]
    unnamed x1 -> x6, local copies, waits for them, and re-layouts: 1.87 us -> 2.07 us
where the time goes in v4:
time: 96.1 us; the launch traced here: 95.9 us
  Pallas kernels  93 us (97%)
  local copies, waits for them, and re-layouts  2.07 us (2%)
    pallas_call x1, Pallas kernels, local(): pl.pallas_call(kernel, out_shape=(jax.ShapeDtypeStruct((BLK * NY * NG, D)...  93 us
    unnamed x6, local copies, waits for them, and re-layouts  2.07 us

profile of v4, /device:TPU:1, one launch (start us, length us, event | category | flops | bytes accessed | tf_op | source)
XLA Modules:
  0.0 95.9 jit_solution(18425604067132632844)
XLA Ops:
  0.0 0.0 copy-start
  0.0 0.8 copy-done
  0.8 0.0 copy-start.1
  0.8 0.7 copy-done.1
  1.4 0.0 copy-start.2
  1.4 0.7 copy-done.2
  2.1 93.0 %table_mean.1 = (f32[1024,128]{1,0:T(8,128)S(1)}, f32[8,128]{1,0:T(8,128)S(1)}) custom-call(f32[8192,128]{1,0:T(8,128)} %bitcast.11, s32[64,128]{1,0:T(8,128)S(1)} %bitcast.8, s32[1,64]{1,0:T(1,128)S(1)} %bitcast.9, s32[1,64]{1,0:T(1,128)S(1)} %bitcast.10), custom_call_target="tpu_custom_call" | custom-call | tf_op jit(solution)/shard_map/table_mean/pallas_call | solution.py:303
  95.1 0.8 broadcast_multiply_fusion
  (1 shorter events, 0.0 us)
Async XLA Ops:
  0.0 0.8 copy-start
  0.8 0.7 copy-start.1
  1.4 0.7 copy-start.2
